TPU v7x, 32 devices: a whole 2x2x4 slice. The times are simulated.
32 devices in a mesh: heads: 4 (over y, x), seq: 8 (over z, core).
Axes of the slice: x: 2, y: 2, z: 4, core: 2. Of those that a mesh axis runs over, the one named last changes fastest.
Arguments:
- query: bfloat16 [24, 128, 576], P(None, 'heads'), may hold values from -1024 to 1024
- cache: bfloat16 [4096, 576], P('seq'), may hold values from -8 to 8
- segments: int32 [4096], P('seq'), may hold values from 0 to 3, as said below
- groups: int32 [24], replicated, may hold values from 0 to 3
- value_up: bfloat16 [128, 512, 128], P('heads'), may hold values from -3 to 3
- out_proj: bfloat16 [16384, 7168], P('heads', 'seq'), may hold values from -0.046875 to 0.046875
- targets: float32 [24, 7168], P(None, 'seq'), may hold values from -20 to 20
Outputs:
- projected: float32 [24, 7168], P(None, 'seq')
- loss: float32 [], replicated
- query_grad: float32 [24, 128, 576], P(None, 'heads')
- cache_grad: float32 [4096, 576], P('seq', 'heads')
Inputs may be any that keep to these rules, and one draw needn't show every extreme that they name: `segments`: constant over each aligned tile of 128 cached tokens; every group number appears in some tile.
All inputs are finite; a program needn't handle non-finite values.
Results may differ from a plain program's by a relative error of at most 0.015.
Values may be sent and summed in bfloat16 or wider, within the bound.
No kernel may reach another device: no remote copies, remote signals or barrier semaphores. Data moves between devices by JAX's collectives and lax.ppermute only.
A program may use at most 64 MiB of HBM per device.

v0:
```python
import jax
import jax.numpy as jnp
from jax import lax
from jax.sharding import PartitionSpec as P

scale_factor = 0.07216878364870322
floor_value = -1e30


def on_device(query, cache, segments, groups, value_up, out_proj, targets):
    query_len, head_count, width = query.shape
    latent = value_up.shape[1]
    vwidth = value_up.shape[2]
    row_count = query_len * head_count
    cache_len = cache.shape[0]
    query_rows = query.reshape(row_count, width)
    values = cache[:, :latent]
    allowed = groups[:, None] == segments[None, :]
    allowed_rows = jnp.broadcast_to(
        allowed[:, None, :], (query_len, head_count, cache_len)
    ).reshape(row_count, cache_len)
    scores = (
        jnp.einsum("rc,tc->rt", query_rows, cache, preferred_element_type=jnp.float32)
        * scale_factor
    )
    masked = jnp.where(allowed_rows, scores, floor_value)
    local_top = jnp.max(masked, axis=1)
    maximum = lax.pmax(local_top, "seq")
    weights = jnp.where(allowed_rows, jnp.exp(masked - maximum[:, None]), 0.0)
    totals = lax.psum(jnp.sum(weights, axis=1), "seq")
    partial_latent = jnp.dot(
        weights.astype(jnp.bfloat16), values, preferred_element_type=jnp.float32
    )
    portion = lax.psum_scatter(partial_latent, "seq", scatter_dimension=0, tiled=True)
    share_rows = portion.shape[0]
    start = lax.axis_index("seq") * share_rows
    share_totals = lax.dynamic_slice_in_dim(totals, start, share_rows)
    share_latent = (portion / share_totals[:, None]).astype(jnp.bfloat16)
    head_ids = (start + jnp.arange(share_rows, dtype=jnp.int32)) % head_count
    row_weights = jnp.take(value_up, head_ids, axis=0)
    share_value = jnp.einsum(
        "rc,rcv->rv", share_latent, row_weights, preferred_element_type=jnp.float32
    ).astype(jnp.bfloat16)
    value_out = lax.all_gather(share_value, "seq", axis=0, tiled=True).reshape(
        query_len, head_count, vwidth
    )
    flattened = value_out.reshape(query_len, head_count * vwidth)
    partial_proj = jnp.dot(flattened, out_proj, preferred_element_type=jnp.float32)
    projected = lax.psum(partial_proj, "heads")
    residual = projected - targets
    square_part = jnp.sum(residual * residual)
    model_width = targets.shape[1] * lax.axis_size("seq")
    d_projected = residual.astype(jnp.bfloat16)
    value_partial = jnp.einsum(
        "qd,rd->qr", d_projected, out_proj, preferred_element_type=jnp.float32
    )
    d_value = lax.psum(value_partial, "seq").reshape(query_len, head_count, vwidth)
    d_latent = (
        jnp.einsum(
            "qhv,hcv->qhc",
            d_value.astype(jnp.bfloat16),
            value_up,
            preferred_element_type=jnp.float32,
        )
        .astype(jnp.bfloat16)
        .reshape(row_count, latent)
    )
    row_dot = jnp.sum(d_value * value_out.astype(jnp.float32), axis=2).reshape(row_count)
    probs = weights / totals[:, None]
    d_probs = jnp.einsum("rc,tc->rt", d_latent, values, preferred_element_type=jnp.float32)
    d_scores = (scale_factor * probs * (d_probs - row_dot[:, None])).astype(jnp.bfloat16)
    query_part = jnp.dot(d_scores, cache, preferred_element_type=jnp.float32)
    square_total = lax.psum(square_part, "seq")
    query_sum = lax.psum(query_part, "seq")
    loss = square_total / (query_len * model_width)
    query_grad = query_sum.reshape(query_len, head_count, width)
    key_part = jnp.einsum("rt,rc->tc", d_scores, query_rows, preferred_element_type=jnp.float32)
    value_part = jnp.einsum(
        "rt,rc->tc", probs.astype(jnp.bfloat16), d_latent, preferred_element_type=jnp.float32
    )
    cache_part = key_part + jnp.concatenate(
        [value_part, jnp.zeros((cache_len, width - latent), jnp.float32)], axis=1
    )
    cache_grad = lax.psum_scatter(
        cache_part.astype(jnp.bfloat16), "heads", scatter_dimension=1, tiled=True
    ).astype(jnp.float32)
    return (projected, loss, query_grad, cache_grad)


def solution(mesh):
    in_specs = (
        P(None, "heads", None),
        P("seq", None),
        P("seq"),
        P(),
        P("heads", None, None),
        P("heads", "seq"),
        P(None, "seq"),
    )
    out_specs = (P(None, "seq"), P(), P(None, "heads", None), P("seq", "heads"))
    return jax.shard_map(
        on_device, mesh=mesh, in_specs=in_specs, out_specs=out_specs, check_vma=False
    )
```

profile of v0, /device:TPU:0, one launch (start us, length us, event | category | flops | bytes accessed | tf_op | source)
XLA Modules:
  0.0 309.5 jit_solution(6097966343069492329)
XLA Ops:
  7.2 0.8 broadcast_compare_fusion
  8.7 2.0 fusion.25
  10.7 18.1 %pmax.7 = f32[768]{0:T(1024)S(1)} all-reduce(f32[768]{0:T(1024)S(1)} %get-tuple-element.4), channel_id=1, replica_groups=mesh['heads'=4,'seq'=8] {'seq'}, use_global_device_ids=true, to_apply=%region_1.2 | all-reduce | flops 768 | bytes 6144 | tf_op jit(solution)/shard_map/pmax | solution.py:28
  28.8 1.8 fusion.8
  31.1 13.7 %psum.35 = f32[768]{0:T(1024)S(1)} all-reduce(f32[768]{0:T(1024)S(1)} %fusion.15), channel_id=1, replica_groups=mesh['heads'=4,'seq'=8] {'seq'}, use_global_device_ids=true, to_apply=%region_4.5 | all-reduce | flops 768 | bytes 6144 | tf_op jit(solution)/shard_map/psum | solution.py:30
  45.4 8.8 %gather_fusion = bf16[96,512,128]{2,1,0:T(8,128)(2,1)} fusion(bf16[32,512,128]{2,1,0:T(8,128)(2,1)} %param.11, s32[1024]{0:T(1024)S(1)} %pad_clamp_fusion), kind=kCustom, calls=%fused_computation | custom fusion | bytes 25166208 | tf_op jit(solution)/shard_map/jit(_take)/gather | solution.py:40
  54.2 9.3 %reduce-scatter.3.cloned.1.call-done = f32[96,512]{1,0:T(8,128)} async-done(((f32[768,512]{1,0:T(8,128)}), f32[96,512]{1,0:T(8,128)}) %reduce-scatter.3.cloned.1.call-update) | async-done | bytes 196624 | tf_op jit(solution)/shard_map/reduce_scatter | solution.py:34
  63.5 1.0 fusion.16
  64.5 5.7 %fusion = f32[96,1,128]{2,1,0:T(1,128)S(1)} fusion(bf16[96,512,128]{2,1,0:T(8,128)(2,1)} %gather_fusion, pred[96]{0:T(512)(128)(4,1)S(1)} %compare_and_fusion, bf16[96,512,1]{1,0,2:T(8,128)(2,1)S(1)} %fusion.16), kind=kOutput, calls=%fused_computation.1 | convolution fusion | flops 18874368 | bytes 12730464 | tf_op jit(solution)/shard_map/rc,rcv->rv/dot_general | solution.py:41
  70.3 15.2 %all_gather.3 = bf16[768,128]{1,0:T(8,128)(2,1)} all-gather(bf16[96,128]{1,0:T(8,128)(2,1)S(1)} %convert_element_type.41), channel_id=1, replica_groups=mesh['heads'=4,'seq'=8] {'seq'}, dimensions={0}, use_global_device_ids=true | all-gather | bytes 221184 | tf_op jit(solution)/shard_map/all_gather | solution.py:44
  85.4 1.7 reshape_reshape.3
  87.1 4.9 %fusion.26 = f32[24,896]{1,0:T(8,128)} fusion(bf16[24,4096]{1,0:T(8,128)(2,1)} %reshape_reshape.3, bf16[4096,896]{1,0:T(8,128)(2,1)} %param.12), kind=kOutput, calls=%fused_computation.49 | convolution fusion | flops 176160768 | bytes 7622656 | tf_op jit(solution)/shard_map/dot_general | solution.py:48
  92.1 39.5 %all-reduce.5.cloned.1.call-done = f32[24,896]{1,0:T(8,128)} async-done(((f32[24,896]{1,0:T(8,128)}), f32[24,896]{1,0:T(8,128)}) %all-reduce.5.cloned.1.call-update) | async-done | bytes 86032 | tf_op jit(solution)/shard_map/psum | solution.py:49
  131.6 5.5 %convolution_bitcast_fusion = f32[3,32,8,128]{3,2,1,0:T(8,128)S(1)} fusion(bf16[4096,896]{1,0:T(8,128)(2,1)} %param.12, f32[24,896]{1,0:T(8,128)} %all-reduce.5.cloned.1.call-done, f32[24,896]{1,0:T(8,128)} %param.13), kind=kOutput, calls=%fused_computation.12 | convolution fusion | flops 176203776 | bytes 7905280 | tf_op jit(solution)/shard_map/qd,rd->qr/dot_general | solution.py:54
  137.1 0.8 copy.47
  138.0 1.7 convert.1
  139.7 54.9 %all-reduce.7.cloned.1.call-done = f32[24,32,128]{2,0,1:T(8,128)} async-done(((f32[24,32,128]{2,0,1:T(8,128)}), f32[24,32,128]{2,0,1:T(8,128)}) %all-reduce.7.cloned.1.call-update) | async-done | bytes 393232 | tf_op jit(solution)/shard_map/psum | solution.py:57
  194.6 1.4 fusion.12
  196.0 0.7 copy.33
  196.7 0.8 sub.24
  197.5 4.6 %fusion.5 = bf16[24,32,512]{2,0,1:T(8,128)(2,1)S(1)} fusion(bf16[32,512,128]{2,1,0:T(8,128)(2,1)} %param.11, f32[24,32,128]{2,0,1:T(8,128)} %all-reduce.7.cloned.1.call-done), kind=kOutput, calls=%fused_computation.11 | convolution fusion | flops 101154816 | bytes 5373952 | tf_op jit(solution)/shard_map/qhv,hcv->qhc/dot_general | solution.py:59
  202.8 0.8 fusion.6
  203.5 0.9 multiply_convert_fusion
  204.4 0.9 copy-done.1
  205.3 1.5 fusion.4
  206.9 3.2 %fusion.27 = f32[768,576]{1,0:T(8,128)} fusion(bf16[768,512]{0,1:T(8,128)(2,1)} %copy-done.1, bf16[512,576]{0,1:T(8,128)(2,1)S(1)} %copy-done.2), kind=kOutput, calls=%fused_computation.50 | convolution fusion | flops 452984832 | bytes 3145728 | tf_op jit(solution)/shard_map/dot_general | solution.py:72
  210.1 0.9 copy-done.3
  211.6 14.3 %psum.37 = f32[]{:T(128)} all-reduce(f32[]{:T(128)} %multiply_reduce_fusion), channel_id=1, replica_groups=mesh['heads'=4,'seq'=8] {'seq'}, use_global_device_ids=true, to_apply=%region_7.8 | all-reduce | flops 1 | bytes 8 | tf_op jit(solution)/shard_map/psum | solution.py:73
  226.6 4.8 %reduce-scatter.5.cloned.1.call-done = bf16[512,144]{0,1:T(8,128)(2,1)} async-done(((bf16[512,576]{0,1:T(8,128)(2,1)}), bf16[512,144]{0,1:T(8,128)(2,1)}) %reduce-scatter.5.cloned.1.call-update) | async-done | bytes 147472 | tf_op jit(solution)/shard_map/reduce_scatter | solution.py:84
  231.4 1.7 convert_element_type.51
  233.1 65.2 %all-reduce.9.cloned.1.call-done = f32[24,32,576]{2,1,0:T(8,128)} async-done(((f32[24,32,576]{2,1,0:T(8,128)}), f32[24,32,576]{2,1,0:T(8,128)}) %all-reduce.9.cloned.1.call-update) | async-done | bytes 1769488 | tf_op jit(solution)/shard_map/psum | solution.py:74
  298.9 2.9 copy.57
  (37 shorter events, 3.9 us)
Async XLA Ops:
  7.2 1.5 copy-start
  7.2 56.3 %reduce-scatter.3.cloned.1.call-start = ((), (), s32[]{:S(2)}) async-start(), calls=%async_computation.2 | async-start | bytes 1769472 | tf_op jit(solution)/shard_map/reduce_scatter | solution.py:34
  8.7 20.1 %copy-start.2 = (bf16[512,576]{0,1:T(8,128)(2,1)S(1)}, bf16[512,576]{0,1:T(8,128)(2,1)}, u32[]{:S(2)}) copy-start(bf16[512,576]{0,1:T(8,128)(2,1)} %param.8) | copy-start | bytes 1769476
  28.8 1.9 copy-start.5
  30.6 101.0 %all-reduce.5.cloned.1.call-start = ((), (), s32[]{:S(2)}) async-start(), calls=%async_computation.3 | async-start | bytes 172032 | tf_op jit(solution)/shard_map/psum | solution.py:49
  44.8 0.6 copy-start.7
  92.0 102.6 %all-reduce.7.cloned.1.call-start = ((), (), s32[]{:S(2)}) async-start(), calls=%async_computation.4 | async-start | bytes 786432 | tf_op jit(solution)/shard_map/psum | solution.py:57
  137.9 93.5 %reduce-scatter.5.cloned.1.call-start = ((), (), s32[]{:S(2)}) async-start(), calls=%async_computation.6 | async-start | bytes 737280 | tf_op jit(solution)/shard_map/reduce_scatter | solution.py:84
  202.1 0.7 copy-start.6
  202.1 0.7 copy-start.8
  204.4 0.9 copy-start.1
  206.8 91.4 %all-reduce.9.cloned.1.call-start = ((), (), s32[]{:S(2)}) async-start(), calls=%async_computation.5 | async-start | bytes 3932160 | tf_op jit(solution)/shard_map/psum | solution.py:74
  210.1 0.9 copy-start.3
  210.1 0.9 copy-start.4
Sparse Core Ops, SparseCore 0:
  30.8 32.6 reduce-scatter.2
  92.2 39.4 all-reduce.4
  138.0 56.5 all-reduce.6
  206.9 24.4 reduce-scatter.4
  234.2 63.9 all-reduce.8
where the time goes:
time: 310 us; the launch traced here: 309 us
  waiting for transfers between devices  174 us (56%)
  blocking collectives  61.3 us (20%)
  matrix products  30.8 us (10%)
  local copies, waits for them, and re-layouts  19.9 us (6%)
  between operations  15.7 us (5%)
  other arithmetic  7.67 us (2%)
    psum x1, waiting for transfers between devices, on_device(): query_sum = lax.psum(query_part, 'seq')  65.2 us
    psum x1, waiting for transfers between devices, on_device(): lax.psum(value_partial, 'seq').reshape(query_len, head_count, vwidth)  54.9 us
    psum x1, waiting for transfers between devices, on_device(): projected = lax.psum(partial_proj, 'heads')  39.5 us
    pmax x1, blocking collectives, on_device(): maximum = lax.pmax(local_top, 'seq')  18.1 us
    all_gather x1, blocking collectives, on_device(): lax.all_gather(share_value, 'seq', axis=0, tiled=True)  15.2 us
    psum x1, blocking collectives, on_device(): square_total = lax.psum(square_part, 'seq')  14.3 us
    psum x1, blocking collectives, on_device(): totals = lax.psum(jnp.sum(weights, axis=1), 'seq')  13.7 us
    reduce_scatter x1, waiting for transfers between devices, on_device(): lax.psum_scatter(partial_latent, 'seq', scatter_dimension=0, tiled=True)  9.28 us
  transfers between devices with their start and end apart: 5, of which 5 were waited for; matrix products, arithmetic and copies ran while one was open for 5% of the time, Pallas kernels for 0%

commit v1 on v0

--- a/solution.py
+++ b/solution.py
@@ -71,7 +71,11 @@
     d_scores = (scale_factor * probs * (d_probs - row_dot[:, None])).astype(jnp.bfloat16)
     query_part = jnp.dot(d_scores, cache, preferred_element_type=jnp.float32)
     square_total = lax.psum(square_part, "seq")
-    query_sum = lax.psum(query_part, "seq")
+    query_sum = query_part
+    for hop in (1, 2, 4):
+        query_sum = query_sum + lax.ppermute(
+            query_sum, "seq", [(dev, dev ^ hop) for dev in range(8)]
+        )
     loss = square_total / (query_len * model_width)
     query_grad = query_sum.reshape(query_len, head_count, width)
     key_part = jnp.einsum("rt,rc->tc", d_scores, query_rows, preferred_element_type=jnp.float32)

time: 310 us -> 344 us (1.11); the launches traced: 309 us -> 338 us
  blocking collectives: 61.3 us -> 92.5 us
  local copies, waits for them, and re-layouts: 19.9 us -> 14 us
    ppermute x0 -> x3, waiting for transfers between devices: none -> 69.3 us  [on_device(): lax.ppermute(query_sum, 'seq', [(dev, dev ^ hop) for dev in range(8)])]
    psum x1 -> x0, waiting for transfers between devices: 65.2 us -> none  [on_device(): query_sum = lax.psum(query_part, 'seq')]
    psum x1, blocking collectives: 14.3 us -> 46.6 us  [on_device(): square_total = lax.psum(square_part, 'seq')]
    unnamed x20 -> x17, local copies, waits for them, and re-layouts: 6.34 us -> 1.49 us
    reduce_scatter x1, waiting for transfers between devices: 4.83 us -> 0.02 us  [on_device(): lax.psum_scatter(cache_part.astype(jnp.bfloat16), 'heads', scatter_dimens...]
  transfers between devices with their start and end apart: 5 -> 7, of which waited for: 5 -> 6; matrix products, arithmetic and copies ran while one was open for 5% -> 4% of each run, Pallas kernels for 0% -> 0%
where the time goes in v1:
time: 344 us; the launch traced here: 338 us
  waiting for transfers between devices  175 us (51%)
  blocking collectives  92.5 us (27%)
  matrix products  29.1 us (8%)
  between operations  15.8 us (5%)
  local copies, waits for them, and re-layouts  14 us (4%)
  other arithmetic  8.53 us (2%)
    ppermute x3, waiting for transfers between devices, on_device(): lax.ppermute(query_sum, 'seq', [(dev, dev ^ hop) for dev in range(8)])  69.3 us
    psum x1, waiting for transfers between devices, on_device(): lax.psum(value_partial, 'seq').reshape(query_len, head_count, vwidth)  56.4 us
    psum x1, blocking collectives, on_device(): square_total = lax.psum(square_part, 'seq')  46.6 us
    psum x1, waiting for transfers between devices, on_device(): projected = lax.psum(partial_proj, 'heads')  40 us
    pmax x1, blocking collectives, on_device(): maximum = lax.pmax(local_top, 'seq')  18.1 us
    all_gather x1, blocking collectives, on_device(): lax.all_gather(share_value, 'seq', axis=0, tiled=True)  14.1 us
    psum x1, blocking collectives, on_device(): totals = lax.psum(jnp.sum(weights, axis=1), 'seq')  13.7 us
    reduce_scatter x1, waiting for transfers between devices, on_device(): lax.psum_scatter(partial_latent, 'seq', scatter_dimension=0, tiled=True)  9.48 us
  transfers between devices with their start and end apart: 7, of which 6 were waited for; matrix products, arithmetic and copies ran while one was open for 4% of the time, Pallas kernels for 0%

profile of v1, /device:TPU:0, one launch (start us, length us, event | category | flops | bytes accessed | tf_op | source)
XLA Modules:
  0.0 337.8 jit_solution(2503684157358747362)
XLA Ops:
  7.2 0.8 broadcast_compare_fusion
  8.7 1.9 fusion.25
  10.6 18.1 %pmax.7 = f32[768]{0:T(1024)S(1)} all-reduce(f32[768]{0:T(1024)S(1)} %get-tuple-element.8), channel_id=1, replica_groups=mesh['heads'=4,'seq'=8] {'seq'}, use_global_device_ids=true, to_apply=%region_1.2 | all-reduce | flops 768 | bytes 6144 | tf_op jit(solution)/shard_map/pmax | solution.py:28
  28.8 2.8 fusion.8
  32.0 13.7 %psum.28 = f32[768]{0:T(1024)S(1)} all-reduce(f32[768]{0:T(1024)S(1)} %fusion.15), channel_id=1, replica_groups=mesh['heads'=4,'seq'=8] {'seq'}, use_global_device_ids=true, to_apply=%region_4.5 | all-reduce | flops 768 | bytes 6144 | tf_op jit(solution)/shard_map/psum | solution.py:30
  45.8 8.8 %gather_fusion = bf16[96,512,128]{2,1,0:T(8,128)(2,1)} fusion(bf16[32,512,128]{2,1,0:T(8,128)(2,1)} %param.11, s32[1024]{0:T(1024)S(1)} %pad_clamp_fusion), kind=kCustom, calls=%fused_computation | custom fusion | bytes 25166208 | tf_op jit(solution)/shard_map/jit(_take)/gather | solution.py:40
  54.6 9.5 %reduce-scatter.3.cloned.1.call-done = f32[96,512]{1,0:T(8,128)} async-done(((f32[768,512]{1,0:T(8,128)}), f32[96,512]{1,0:T(8,128)}) %reduce-scatter.3.cloned.1.call-update) | async-done | bytes 196624 | tf_op jit(solution)/shard_map/reduce_scatter | solution.py:34
  64.1 1.0 fusion.16
  65.1 5.8 %fusion = f32[96,1,128]{2,1,0:T(1,128)S(1)} fusion(bf16[96,512,128]{2,1,0:T(8,128)(2,1)} %gather_fusion, pred[96]{0:T(512)(128)(4,1)S(1)} %compare_and_fusion, bf16[96,512,1]{1,0,2:T(8,128)(2,1)S(1)} %fusion.16), kind=kOutput, calls=%fused_computation.1 | convolution fusion | flops 18874368 | bytes 12730464 | tf_op jit(solution)/shard_map/rc,rcv->rv/dot_general | solution.py:41
  70.9 14.1 %all_gather.3 = bf16[768,128]{1,0:T(8,128)(2,1)S(1)} all-gather(bf16[96,128]{1,0:T(8,128)(2,1)S(1)} %convert_element_type.41), channel_id=1, replica_groups=mesh['heads'=4,'seq'=8] {'seq'}, dimensions={0}, use_global_device_ids=true | all-gather | bytes 221184 | tf_op jit(solution)/shard_map/all_gather | solution.py:44
  85.1 4.8 %fusion.26 = f32[24,896]{1,0:T(8,128)} fusion(bf16[24,4096]{1,0:T(8,128)(2,1)S(1)} %reshape_reshape.3, bf16[4096,896]{1,0:T(8,128)(2,1)} %param.12), kind=kOutput, calls=%fused_computation.49 | convolution fusion | flops 176160768 | bytes 7622656 | tf_op jit(solution)/shard_map/dot_general | solution.py:48
  90.0 40.0 %all-reduce.4.cloned.1.call-done = f32[24,896]{1,0:T(8,128)} async-done(((f32[24,896]{1,0:T(8,128)}), f32[24,896]{1,0:T(8,128)}) %all-reduce.4.cloned.1.call-update) | async-done | bytes 86032 | tf_op jit(solution)/shard_map/psum | solution.py:49
  130.0 5.4 %convolution_bitcast_fusion = f32[3,32,8,128]{3,2,1,0:T(8,128)S(1)} fusion(bf16[4096,896]{1,0:T(8,128)(2,1)} %param.12, f32[24,896]{1,0:T(8,128)} %all-reduce.4.cloned.1.call-done, f32[24,896]{1,0:T(8,128)S(1)} %copy-done.6), kind=kOutput, calls=%fused_computation.12 | convolution fusion | flops 176203776 | bytes 7905280 | tf_op jit(solution)/shard_map/qd,rd->qr/dot_general | solution.py:54
  135.4 0.8 copy.46
  136.5 56.4 %all-reduce.6.cloned.1.call-done = f32[24,32,128]{2,0,1:T(8,128)} async-done(((f32[24,32,128]{2,0,1:T(8,128)}), f32[24,32,128]{2,0,1:T(8,128)}) %all-reduce.6.cloned.1.call-update) | async-done | bytes 393232 | tf_op jit(solution)/shard_map/psum | solution.py:57
  192.9 1.3 fusion.12
  194.4 4.6 %fusion.5 = bf16[24,32,512]{2,0,1:T(8,128)(2,1)S(1)} fusion(bf16[32,512,128]{2,1,0:T(8,128)(2,1)} %param.11, f32[24,32,128]{2,0,1:T(8,128)} %all-reduce.6.cloned.1.call-done), kind=kOutput, calls=%fused_computation.11 | convolution fusion | flops 101154816 | bytes 5373952 | tf_op jit(solution)/shard_map/qhv,hcv->qhc/dot_general | solution.py:59
  199.3 0.8 copy-done.4
  200.1 0.8 multiply_convert_fusion
  200.9 0.6 fusion.27
  201.6 3.7 %collective-permute-done = f32[768,576]{0,1:T(8,128)S(1)} collective-permute-done((f32[768,576]{0,1:T(8,128)S(1)}, f32[768,576]{0,1:T(8,128)S(1)}, u32[]{:S(2)}, u32[]{:S(2)}) %collective-permute-start) | collective-permute-done | bytes 1769504 | tf_op jit(solution)/shard_map/ppermute | solution.py:76
  206.2 40.1 %collective-permute-done.1 = f32[768,576]{0,1:T(8,128)S(1)} collective-permute-done((f32[768,576]{0,1:T(8,128)S(1)}, f32[768,576]{0,1:T(8,128)S(1)}, u32[]{:S(2)}, u32[]{:S(2)}) %collective-permute-start.1) | collective-permute-done | bytes 1769504 | tf_op jit(solution)/shard_map/ppermute | solution.py:76
  246.5 1.5 collective-permute-start.2
  248.0 0.8 fusion.6
  248.8 1.5 fusion.4
  250.4 0.6 multiply_reduce_fusion
  251.0 46.6 %psum.30 = f32[]{:T(128)} all-reduce(f32[]{:T(128)} %multiply_reduce_fusion), channel_id=1, replica_groups=mesh['heads'=4,'seq'=8] {'seq'}, use_global_device_ids=true, to_apply=%region_7.8 | all-reduce | flops 1 | bytes 8 | tf_op jit(solution)/shard_map/psum | solution.py:73
  298.3 1.7 convert_element_type.51
  300.0 25.5 %collective-permute-done.2 = f32[768,576]{0,1:T(8,128)} collective-permute-done((f32[768,576]{0,1:T(8,128)S(1)}, f32[768,576]{0,1:T(8,128)}, u32[]{:S(2)}, u32[]{:S(2)}) %collective-permute-start.2) | collective-permute-done | bytes 1769504 | tf_op jit(solution)/shard_map/ppermute | solution.py:76
  325.5 2.2 add.93
  327.7 1.8 copy.35
  329.5 0.6 copy.54
  (41 shorter events, 3.2 us)
Async XLA Ops:
  7.2 1.5 copy-start
  7.2 56.9 %reduce-scatter.3.cloned.1.call-start = ((), (), s32[]{:S(2)}) async-start(), calls=%async_computation.2 | async-start | bytes 1769472 | tf_op jit(solution)/shard_map/reduce_scatter | solution.py:34
  10.6 188.6 %copy-start.2 = (f32[768,512]{0,1:T(8,128)}, f32[768,512]{0,1:T(8,128)S(1)}, u32[]{:S(2)}) copy-start(f32[768,512]{0,1:T(8,128)S(1)} %get-tuple-element.9) | copy-start | bytes 4718596
  31.6 98.4 %all-reduce.4.cloned.1.call-start = ((), (), s32[]{:S(2)}) async-start(), calls=%async_computation.3 | async-start | bytes 172032 | tf_op jit(solution)/shard_map/psum | solution.py:49
  85.1 44.9 %copy-start.6 = (f32[24,896]{1,0:T(8,128)S(1)}, f32[24,896]{1,0:T(8,128)}, u32[]{:S(2)}) copy-start(f32[24,896]{1,0:T(8,128)} %param.13) | copy-start | bytes 258052
  90.0 103.0 %all-reduce.6.cloned.1.call-start = ((), (), s32[]{:S(2)}) async-start(), calls=%async_computation.4 | async-start | bytes 786432 | tf_op jit(solution)/shard_map/psum | solution.py:57
  136.2 162.1 %reduce-scatter.5.cloned.1.call-start = ((), (), s32[]{:S(2)}) async-start(), calls=%async_computation.5 | async-start | bytes 737280 | tf_op jit(solution)/shard_map/reduce_scatter | solution.py:88
  199.0 1.1 copy-start.4
  201.6 3.8 %collective-permute-start = (f32[768,576]{0,1:T(8,128)S(1)}, f32[768,576]{0,1:T(8,128)S(1)}, u32[]{:S(2)}, u32[]{:S(2)}) collective-permute-start(f32[768,576]{0,1:T(8,128)S(1)} %fusion.27), channel_id=1, source_target_pairs={{0,1},{1,0},{2,3},{3,2},{4,5},{5,4},{6,7},{7,6},{8,9},{9,8},{10,11... | collective-permute-start | bytes 5308424 | tf_op jit(solution)/shard_map/ppermute | solution.py:76
  205.5 42.5 %copy-start.3 = (f32[768,512]{0,1:T(8,128)S(1)}, f32[768,512]{0,1:T(8,128)}, u32[]{:S(2)}) copy-start(f32[768,512]{0,1:T(8,128)} %copy-done.2) | copy-start | bytes 4718596
  205.6 40.7 %collective-permute-start.1 = (f32[768,576]{0,1:T(8,128)S(1)}, f32[768,576]{0,1:T(8,128)S(1)}, u32[]{:S(2)}, u32[]{:S(2)}) collective-permute-start(f32[768,576]{0,1:T(8,128)S(1)} %add.91), channel_id=1, source_target_pairs={{0,2},{1,3},{2,0},{3,1},{4,6},{5,7},{6,4},{7,5},{8,10},{9,11},{10,... | collective-permute-start | bytes 5308424 | tf_op jit(solution)/shard_map/ppermute | solution.py:76
  246.5 2.3 copy-start.1
  246.5 79.0 %collective-permute-start.2 = (f32[768,576]{0,1:T(8,128)S(1)}, f32[768,576]{0,1:T(8,128)}, u32[]{:S(2)}, u32[]{:S(2)}) collective-permute-start(f32[768,576]{0,1:T(8,128)S(1)} %add.92), channel_id=1, source_target_pairs={{0,4},{1,5},{2,6},{3,7},{4,0},{5,1},{6,2},{7,3},{8,12},{9,13},{10,... | collective-permute-start | bytes 5308424 | tf_op jit(solution)/shard_map/ppermute | solution.py:76
  248.8 1.6 copy-start.5
  248.8 1.6 copy-start.7
Sparse Core Ops, SparseCore 0:
  31.7 32.3 reduce-scatter.2
  90.1 39.8 all-reduce.3
  136.4 56.5 all-reduce.5
  250.5 24.4 reduce-scatter.4
